TPU v7x, 256 devices: a 8x8x2 block of a 8x8x16 slice. The times are simulated.
256 devices in a mesh: groups: 2 (over z), adapter: 16 (over x, core), tensor: 8 (over y).
Axes of the slice: x: 8, y: 8, z: 2, core: 2. Of those that a mesh axis runs over, the one named last changes fastest.
The devices are a block of a 8x8x16 slice.
Arguments:
- tokens: bfloat16 [8192, 8192], P(('groups', 'adapter'), 'tensor'), parts along dimension 0, may hold values from -6 to 6
- query_weight: bfloat16 [8192, 8192], P('tensor', 'adapter'), may hold values from -0.0625 to 0.0625
- adapter_down_weight: bfloat16 [512, 16, 8192], P('adapter', None, 'tensor'), may hold values from -0.0625 to 0.0625
- adapter_up_weight: bfloat16 [512, 16, 8192], P('adapter'), may hold values from -1.5 to 1.5
- block_adapter_ids: int32 [64], P('groups'), parts along dimension 0, may hold values from 0 to 511, as said below
- block_live_count: int32 [64], P('groups'), parts along dimension 0, may hold values from 1 to 128
- adapter_slot_index: int32 [1024], P('groups'), parts along dimension 0, may hold values from 0 to 511, as said below
Outputs:
- query: bfloat16 [8192, 8192], P(('groups', 'tensor'), 'adapter'), parts along dimension 0
There are 2 independent parts, one for each index of `groups`. A program takes and returns all parts, laid end to end along the dimension named above; an argument that names none is the same for every part. Nothing has to cross between parts.
Inputs may be any that keep to these rules, and one draw needn't show every extreme that they name: Counting blocks by the owner range adapter_slot_index[block_adapter_ids[k]] // 32, no owner has more than 4 blocks, and one owner has exactly 4 in every draw. `adapter_slot_index`: A permutation: each slot holds exactly one adapter.
All inputs are finite; a program needn't handle non-finite values.
Results may differ from a plain program's by a relative error of at most 0.014.
Values may be sent and summed in bfloat16 or wider, within the bound.
A program may use at most 128 MiB of HBM per device.

v0:
```python
import jax
import jax.numpy as jnp
from jax import lax
from jax.sharding import PartitionSpec as P

BLOCK = 128
adapter_scale = 2.0


def block_plan(block_adapter_ids, adapter_slot_index, owners, adapters_per_device, capacity):
    adapters = adapter_slot_index.shape[0]
    picked = block_adapter_ids[:, None] == jnp.arange(adapters, dtype=jnp.int32)[None, :]
    block_slot_index = jnp.sum(jnp.where(picked, adapter_slot_index[None, :], 0), axis=1)
    owner_of = block_slot_index // adapters_per_device
    local_slot = block_slot_index % adapters_per_device
    hit_table = (owner_of[:, None] == jnp.arange(owners, dtype=jnp.int32)[None, :]).astype(
        jnp.int32
    )
    before = jnp.cumsum(hit_table, axis=0) - hit_table
    order_in = jnp.sum(before * hit_table, axis=1)
    return (owner_of, local_slot, order_in, owner_of * capacity + order_in)


def on_device(
    tokens,
    query_weight,
    adapter_down_weight,
    adapter_up_weight,
    block_adapter_ids,
    block_live_count,
    adapter_slot_index,
):
    owners = lax.axis_size("adapter")
    my_index = lax.axis_index("adapter")
    tok_dev = tokens.shape[0]
    features = tokens.shape[1]
    adapters_per_device = adapter_down_weight.shape[0]
    rank_width = adapter_down_weight.shape[1]
    blocks = block_adapter_ids.shape[0]
    blk_dev = blocks // owners
    capacity = 2 * blk_dev
    token_row_count = tok_dev * owners
    output_columns = query_weight.shape[1]
    owner_of, local_slot, order_in, packed = block_plan(
        block_adapter_ids, adapter_slot_index, owners, adapters_per_device, capacity
    )
    seat_ids = jnp.arange(capacity, dtype=jnp.int32)
    matches = (owner_of[None, :] == my_index) & (order_in[None, :] == seat_ids[:, None])
    filled = jnp.any(matches, axis=1)
    match_int = matches.astype(jnp.int32)
    local_adapter_rows = jnp.sum(match_int * local_slot[None, :], axis=1)
    token_keep_mask = filled.astype(jnp.bfloat16)
    positions = jnp.arange(BLOCK, dtype=jnp.int32)
    up_weight_packed = (
        jnp.take(adapter_up_weight, local_adapter_rows, axis=0) * token_keep_mask[:, None, None]
    )
    up_recv = lax.all_to_all(up_weight_packed, "adapter", split_axis=2, concat_axis=0, tiled=True)
    down_weight_packed = (
        jnp.take(adapter_down_weight, local_adapter_rows, axis=0) * token_keep_mask[:, None, None]
    )
    down_all = lax.all_gather(down_weight_packed, "adapter", axis=0, tiled=True)
    own_packed = lax.dynamic_slice_in_dim(packed, my_index * blk_dev, blk_dev)
    own_live = lax.dynamic_slice_in_dim(block_live_count, my_index * blk_dev, blk_dev)
    down_own = jnp.take(down_all, own_packed, axis=0)
    live_own = (positions[None, :] < own_live[:, None]).astype(jnp.float32)
    shrunk_own = jnp.einsum(
        "ksd,krd->ksr",
        tokens.reshape(blk_dev, BLOCK, features),
        down_own,
        preferred_element_type=jnp.float32,
    )
    shrunk_own = (
        (shrunk_own * live_own[:, :, None]).astype(jnp.bfloat16).reshape(tok_dev, rank_width)
    )
    token_piece = lax.all_gather(tokens, "adapter", axis=0, tiled=True)
    shrunk_piece = lax.all_gather(shrunk_own, "adapter", axis=0, tiled=True)
    query_product = jnp.dot(token_piece, query_weight, preferred_element_type=jnp.float32)
    up_weight_blocks = jnp.take(up_recv, packed, axis=0)
    adapter_output = jnp.einsum(
        "ksr,krf->ksf",
        shrunk_piece.reshape(blocks, BLOCK, rank_width),
        up_weight_blocks,
        preferred_element_type=jnp.float32,
    )
    partial_output = query_product + adapter_scale * adapter_output.reshape(
        token_row_count, output_columns
    )
    summed = lax.psum_scatter(
        partial_output.astype(jnp.bfloat16), "tensor", scatter_dimension=0, tiled=True
    )
    return summed


def solution(mesh):
    placed = (
        P(("groups", "adapter"), "tensor"),
        P("tensor", "adapter"),
        P("adapter", None, "tensor"),
        P("adapter", None, None),
        P("groups"),
        P("groups"),
        P("groups"),
    )
    return jax.shard_map(
        on_device,
        mesh=mesh,
        in_specs=placed,
        out_specs=P(("groups", "tensor"), "adapter"),
        check_vma=False,
    )
```

profile of v0, /device:TPU:513, one launch (start us, length us, event | category | flops | bytes accessed | tf_op | source)
XLA Modules:
  0.0 212.7 jit_solution(3576047556961893171)
XLA Ops:
  6.5 0.0 copy-start
  6.6 0.0 all-gather.5.cloned.1.call-start
  6.6 1.0 select_reduce_fusion
  7.5 0.1 fusion.11
  7.6 0.1 reduce_window_sum.11
  7.7 0.2 select_reduce_fusion.1
  7.9 0.1 fusion.13
  8.0 0.1 select_reduce_fusion.2
  8.1 1.8 gather_fusion
  9.9 0.7 select_multiply_fusion.1
  10.7 0.1 all-gather.5.cloned.1.call-update
  10.7 0.1 all-gather.3.cloned.1.call-start
  10.8 0.7 all-gather.3.cloned.1.call-update
  11.6 4.0 %gather_fusion.2 = bf16[4,16,8192]{2,1,0:T(8,128)(2,1)S(1)} fusion(bf16[32,16,8192]{2,1,0:T(8,128)(2,1)} %param.10, s32[1024]{0:T(1024)S(1)} %pad_clamp_fusion.2), kind=kCustom, calls=%fused_computation.2 | custom fusion | bytes 2097168 | tf_op jit(solution)/shard_map/jit(_take)/gather | solution.py:55
  15.6 0.2 select_multiply_fusion
  15.7 0.0 copy-start.2
  15.7 8.3 %copy.23 = bf16[4,16,8192]{1,0,2:T(4,128)(2,1)} copy(bf16[4,16,8192]{2,1,0:T(8,128)(2,1)S(1)} %select_multiply_fusion) | data formatting | bytes 2097152 | tf_op jit(solution)/shard_map/mul | solution.py:55
  24.0 11.2 %reshape.207 = bf16[16,2,16384]{2,1,0:T(2,128)(2,1)} reshape(bf16[8192,4,16]{2,1,0:T(4,128)(2,1)} %bitcast.48) | data formatting | bytes 2097152
  35.3 23.9 %all-to-all-start = ((bf16[16,2,16384]{2,1,0:T(2,128)(2,1)}), bf16[16,2,16384]{2,1,0:T(2,128)(2,1)S(1)}, u32[]{:S(2)}, u32[]{:S(2)}) async-start(bf16[16,2,16384]{2,1,0:T(2,128)(2,1)} %reshape.207), calls=%async_computation | async-start | bytes 2097152 | tf_op jit(solution)/shard_map/all_to_all | solution.py:57
  59.2 0.1 reduce-scatter.2.cloned.1.call-start
  59.2 0.0 copy-done.2
  59.2 0.1 dynamic_slice.7
  59.3 0.1 compare_and_fusion.2
  59.4 0.1 compare_convert_fusion
  59.5 0.0 copy-start.1
  59.5 27.7 %all-to-all-done = bf16[16,2,16384]{2,1,0:T(2,128)(2,1)S(1)} async-done(((bf16[16,2,16384]{2,1,0:T(2,128)(2,1)}), bf16[16,2,16384]{2,1,0:T(2,128)(2,1)S(1)}, u32[]{:S(2)}, u32[]{:S(2)}) %all-to-all-start) | async-done | bytes 1048608 | tf_op jit(solution)/shard_map/all_to_all | solution.py:57
  87.2 7.6 %reshape.208 = bf16[8192,4,16]{2,1,0:T(4,128)(2,1)} reshape(bf16[16,2,16384]{2,1,0:T(2,128)(2,1)S(1)} %all-to-all-done) | data formatting | bytes 2097152
  94.8 10.8 %copy.28 = bf16[4,16,16,512]{3,1,0,2:T(8,128)(2,1)S(1)} copy(bf16[4,16,16,512]{1,0,3,2:T(4,128)(2,1)} %bitcast.49) | data formatting | bytes 2097152 | tf_op jit(solution)/shard_map/all_to_all | solution.py:57
  105.6 0.6 gather_fusion.3
  106.2 0.0 all-gather.5.cloned.1.call-done
  106.2 2.2 %gather_fusion.1 = bf16[2,16,1024]{2,1,0:T(8,128)(2,1)S(1)} fusion(bf16[64,16,1024]{2,1,0:T(8,128)(2,1)} %all-gather.5.cloned.1.call-done, s32[1024]{0:T(1024)S(1)} %pad_clamp_fusion.1), kind=kCustom, calls=%fused_computation.1 | custom fusion | bytes 131080 | tf_op jit(solution)/shard_map/jit(_take)/gather | solution.py:64
  108.4 0.0 copy-done.1
  108.4 0.3 fusion.2
  108.7 17.2 %all_gather.11 = bf16[4096,16]{0,1:T(8,128)(2,1)S(1)} all-gather(bf16[256,16]{0,1:T(8,128)(2,1)S(1)} %bitcast.52), channel_id=1, replica_groups=mesh['groups'=2,'adapter'=16,'tensor'=8] {'adapter'}, dimensions={0}, use_global_device_ids=true | all-gather | bytes 139264 | tf_op jit(solution)/shard_map/all_gather | solution.py:76
  125.9 4.5 %broadcast_multiply_fusion = f32[32,128,512]{2,1,0:T(8,128)} fusion(bf16[32,16,512]{2,1,0:T(8,128)(2,1)S(1)} %gather_fusion.3, pred[32]{0:T(512)(128)(4,1)S(1)} %get-tuple-element.7, bf16[4096,16]{0,1:T(8,128)(2,1)S(1)} %all_gather.11), kind=kOutput, calls=%fused_computation.6 | convolution fusion | flops 69468160 | bytes 9044000 | tf_op jit(solution)/shard_map/ksr,krf->ksf/dot_general | solution.py:79
  130.4 9.4 %all-gather.3.cloned.1.call-done = bf16[4096,1024]{1,0:T(8,128)(2,1)} async-done(((bf16[256,1024]{1,0:T(8,128)(2,1)}), bf16[4096,1024]{1,0:T(8,128)(2,1)}) %all-gather.3.cloned.1.call-update) | async-done | bytes 8388624 | tf_op jit(solution)/shard_map/all_gather | solution.py:75
  139.8 0.0 copy-done
  139.8 10.7 %fusion = bf16[4096,512]{1,0:T(8,128)(2,1)} fusion(f32[32,128,512]{2,1,0:T(8,128)} %broadcast_multiply_fusion, bf16[4096,1024]{1,0:T(8,128)(2,1)} %all-gather.3.cloned.1.call-done, bf16[1024,512]{1,0:T(8,128)(2,1)S(1)} %copy-done), kind=kOutput, calls=%fused_computation.5 | convolution fusion | flops 4299161600 | bytes 22020096 | tf_op jit(solution)/shard_map/dot_general | solution.py:77
  150.5 0.1 reduce-scatter.2.cloned.1.call-update
  150.6 55.6 %reduce-scatter.2.cloned.1.call-done = bf16[512,512]{1,0:T(8,128)(2,1)} async-done(((bf16[4096,512]{1,0:T(8,128)(2,1)}), bf16[512,512]{1,0:T(8,128)(2,1)}) %reduce-scatter.2.cloned.1.call-update) | async-done | bytes 524304 | tf_op jit(solution)/shard_map/reduce_scatter | solution.py:88
  (11 shorter events, 0.1 us)
Async XLA Ops:
  6.5 133.2 %copy-start = (bf16[1024,512]{1,0:T(8,128)(2,1)S(1)}, bf16[1024,512]{1,0:T(8,128)(2,1)}, u32[]{:S(2)}) copy-start(bf16[1024,512]{1,0:T(8,128)(2,1)} %param.8) | copy-start | bytes 3145732
  6.6 99.6 %all-gather.5.cloned.1.call-start = ((), (), s32[]{:S(2)}) async-start(), calls=%async_computation.3 | async-start | bytes 2228224 | tf_op jit(solution)/shard_map/all_gather | solution.py:61
  10.7 129.0 %all-gather.3.cloned.1.call-start = ((), (), s32[]{:S(2)}) async-start(), calls=%async_computation.2 | async-start | bytes 8912896 | tf_op jit(solution)/shard_map/all_gather | solution.py:75
  15.7 43.5 %copy-start.2 = (s32[32]{0:T(128)S(1)}, s32[32]{0:T(128)}, u32[]{:S(2)}) copy-start(s32[32]{0:T(128)} %param.12) | copy-start | bytes 388
  35.3 51.9 %all-to-all-start = ((bf16[16,2,16384]{2,1,0:T(2,128)(2,1)}), bf16[16,2,16384]{2,1,0:T(2,128)(2,1)S(1)}, u32[]{:S(2)}, u32[]{:S(2)}) async-start(bf16[16,2,16384]{2,1,0:T(2,128)(2,1)} %reshape.207), calls=%async_computation | async-start | bytes 2097152 | tf_op jit(solution)/shard_map/all_to_all | solution.py:57
  59.2 147.0 %reduce-scatter.2.cloned.1.call-start = ((), (), s32[]{:S(2)}) async-start(), calls=%async_computation.4 | async-start | bytes 4718592 | tf_op jit(solution)/shard_map/reduce_scatter | solution.py:88
  59.5 48.9 %copy-start.1 = (bf16[256,1024]{1,0:T(8,128)(2,1)S(1)}, bf16[256,1024]{1,0:T(8,128)(2,1)}, u32[]{:S(2)}) copy-start(bf16[256,1024]{1,0:T(8,128)(2,1)} %param.7) | copy-start | bytes 1572868
Sparse Core Ops, SparseCore 0:
  10.9 65.9 all-gather.4
  78.7 61.0 all-gather.2
  150.7 55.4 reduce-scatter.1
where the time goes:
time: 213 us
  waiting for transfers between devices  93.5 us (44%)
  local copies, waits for them, and re-layouts  46.6 us (22%)
  starting transfers between devices  24 us (11%)
  blocking collectives  17.2 us (8%)
  matrix products  15.5 us (7%)
  between operations  13.3 us (6%)
  other arithmetic  2.65 us (1%)
    reduce_scatter x1, waiting for transfers between devices, on_device(): lax.psum_scatter(partial_output.astype(jnp.bfloat16), 'tensor', scatter_d...  55.6 us
    all_to_all x1, waiting for transfers between devices, on_device(): lax.all_to_all(up_weight_packed, 'adapter', split_axis=2, concat_axis=0,...  27.7 us
    all_to_all x1, starting transfers between devices, on_device(): lax.all_to_all(up_weight_packed, 'adapter', split_axis=2, concat_axis=0,...  23.9 us
    unnamed x8, local copies, waits for them, and re-layouts  18.9 us
    all_gather x1, blocking collectives, on_device(): shrunk_piece = lax.all_gather(shrunk_own, 'adapter', axis=0, tiled=True)  17.2 us
    all_to_all x1, local copies, waits for them, and re-layouts, on_device(): lax.all_to_all(up_weight_packed, 'adapter', split_axis=2, concat_axis=0,...  10.8 us
    dot_general x1, matrix products, on_device(): jnp.dot(token_piece, query_weight, preferred_element_type=jnp.float32)  10.7 us
    all_gather x1, waiting for transfers between devices, on_device(): token_piece = lax.all_gather(tokens, 'adapter', axis=0, tiled=True)  9.36 us
  transfers between devices with their start and end apart: 4, of which 3 were waited for; matrix products, arithmetic and copies ran while one was open for 23% of the time, Pallas kernels for 0%

commit v1 on v0

--- a/solution.py
+++ b/solution.py
@@ -54,7 +54,15 @@
     up_weight_packed = (
         jnp.take(adapter_up_weight, local_adapter_rows, axis=0) * token_keep_mask[:, None, None]
     )
-    up_recv = lax.all_to_all(up_weight_packed, "adapter", split_axis=2, concat_axis=0, tiled=True)
+    up_recv = jnp.concatenate(
+        lax.all_to_all(
+            jnp.stack(jnp.split(up_weight_packed, lax.axis_size("adapter"), axis=2)),
+            "adapter",
+            0,
+            0,
+        ),
+        axis=0,
+    )
     down_weight_packed = (
         jnp.take(adapter_down_weight, local_adapter_rows, axis=0) * token_keep_mask[:, None, None]
     )

time: 213 us -> 215 us (level)
  waiting for transfers between devices: 93.5 us -> 125 us
  local copies, waits for them, and re-layouts: 46.6 us -> 18.5 us
    all_gather x1, waiting for transfers between devices: 9.36 us -> 35.5 us  [on_device(): token_piece = lax.all_gather(tokens, 'adapter', axis=0, tiled=True)]
    all_to_all x1 -> x0, local copies, waits for them, and re-layouts: 10.8 us -> none  [on_device(): lax.all_to_all(up_weight_packed, 'adapter', split_axis=2, concat_axis=0,...]
    unnamed x8 -> x21, local copies, waits for them, and re-layouts: 18.9 us -> 9.34 us
    mul x1 -> x0, local copies, waits for them, and re-layouts: 8.29 us -> none  [on_device(): jnp.take(adapter_up_weight, local_adapter_rows, axis=0)]
    all_to_all x1, waiting for transfers between devices: 27.7 us -> 32.7 us  [on_device(): lax.all_to_all(jnp.stack(jnp.split(up_weight_packed, lax.axis_size('adapt...]
  transfers between devices with their start and end apart: 4 -> 4, of which waited for: 3 -> 3; matrix products, arithmetic and copies ran while one was open for 23% -> 10% of each run, Pallas kernels for 0% -> 0%
where the time goes in v1:
time: 215 us; the launch traced here: 214 us
  waiting for transfers between devices  125 us (58%)
  starting transfers between devices  24 us (11%)
  local copies, waits for them, and re-layouts  18.5 us (9%)
  matrix products  15.6 us (7%)
  blocking collectives  15.4 us (7%)
  between operations  13.3 us (6%)
  other arithmetic  2.68 us (1%)
    reduce_scatter x1, waiting for transfers between devices, on_device(): lax.psum_scatter(partial_output.astype(jnp.bfloat16), 'tensor', scatter_d...  55.6 us
    all_gather x1, waiting for transfers between devices, on_device(): token_piece = lax.all_gather(tokens, 'adapter', axis=0, tiled=True)  35.5 us
    all_to_all x1, waiting for transfers between devices, on_device(): lax.all_to_all(jnp.stack(jnp.split(up_weight_packed, lax.axis_size('adapt...  32.7 us
    all_to_all x1, starting transfers between devices, on_device(): lax.all_to_all(jnp.stack(jnp.split(up_weight_packed, lax.axis_size('adapt...  23.9 us
    all_gather x1, blocking collectives, on_device(): shrunk_piece = lax.all_gather(shrunk_own, 'adapter', axis=0, tiled=True)  15.4 us
    dot_general x1, matrix products, on_device(): jnp.dot(token_piece, query_weight, preferred_element_type=jnp.float32)  10.8 us
    unnamed x21, local copies, waits for them, and re-layouts  9.34 us
    dot_general x1, matrix products, on_device(): jnp.einsum('ksr,krf->ksf', shrunk_piece.reshape(blocks, BLOCK, rank_width...  4.51 us
  transfers between devices with their start and end apart: 4, of which 3 were waited for; matrix products, arithmetic and copies ran while one was open for 10% of the time, Pallas kernels for 0%

profile of v1, /device:TPU:513, one launch (start us, length us, event | category | flops | bytes accessed | tf_op | source)
XLA Modules:
  0.0 214.2 jit_solution(5774402844650574217)
XLA Ops:
  6.5 0.0 copy-start
  6.6 0.0 copy-start.1
  6.6 0.0 copy-start.2
  6.6 0.0 all-gather.5.cloned.1.call-start
  6.6 1.0 select_reduce_fusion
  7.6 0.1 fusion.27
  7.7 0.1 reduce_window_sum.11
  7.7 0.2 select_reduce_fusion.1
  7.9 0.1 fusion.29
  8.0 0.1 select_reduce_fusion.2
  8.2 1.8 gather_fusion
  10.0 0.7 select_multiply_fusion.1
  10.7 0.1 all-gather.5.cloned.1.call-update
  10.8 0.1 all-gather.3.cloned.1.call-start
  10.9 0.7 all-gather.3.cloned.1.call-update
  11.6 4.0 %gather_fusion.2 = bf16[4,16,8192]{2,1,0:T(8,128)(2,1)S(1)} fusion(bf16[32,16,8192]{2,1,0:T(8,128)(2,1)} %param.10, s32[1024]{0:T(1024)S(1)} %pad_clamp_fusion.2), kind=kCustom, calls=%fused_computation.2 | custom fusion | bytes 2097168 | tf_op jit(solution)/shard_map/jit(_take)/gather | solution.py:55
  15.6 0.2 select_multiply_fusion
  15.8 0.6 fusion.23
  16.4 0.6 fusion.22
  17.0 0.6 fusion.21
  17.6 0.6 fusion.20
  18.3 0.6 fusion.19
  18.9 0.6 fusion.18
  19.5 0.6 fusion.17
  20.1 0.6 fusion.16
  20.7 0.6 fusion.15
  21.4 0.6 fusion.14
  22.0 0.6 fusion.13
  22.6 0.6 fusion.12
  23.2 0.6 fusion.11
  23.9 0.6 fusion.10
  24.5 0.6 fusion.9
  25.1 0.6 fusion.8
  25.7 23.9 %all-to-all-start = ((bf16[16,4,16,512]{3,2,1,0:T(8,128)(2,1)}), bf16[16,4,16,512]{3,2,1,0:T(8,128)(2,1)S(1)}, u32[]{:S(2)}, u32[]{:S(2)}) async-start(bf16[16,4,16,512]{3,2,1,0:T(8,128)(2,1)} %fusion.8), calls=%async_computation | async-start | bytes 2097152 | tf_op jit(solution)/shard_map/all_to_all | solution.py:58
  49.6 0.1 reduce-scatter.2.cloned.1.call-start
  49.7 0.0 copy-done.2
  49.7 0.1 dynamic_slice.7
  49.8 0.1 compare_and_fusion.2
  49.9 0.1 compare_convert_fusion
  50.0 32.7 %all-to-all-done = bf16[16,4,16,512]{3,2,1,0:T(8,128)(2,1)S(1)} async-done(((bf16[16,4,16,512]{3,2,1,0:T(8,128)(2,1)}), bf16[16,4,16,512]{3,2,1,0:T(8,128)(2,1)S(1)}, u32[]{:S(2)}, u32[]{:S(2)}) %all-to-all-start) | async-done | bytes 1048608 | tf_op jit(solution)/shard_map/all_to_all | solution.py:58
  82.7 0.6 gather_fusion.3
  83.2 0.0 all-gather.5.cloned.1.call-done
  83.3 2.1 gather_fusion.1
  85.4 0.0 copy-done.1
  85.4 0.3 fusion.2
  85.7 15.4 %all_gather.11 = bf16[4096,16]{0,1:T(8,128)(2,1)S(1)} all-gather(bf16[256,16]{0,1:T(8,128)(2,1)S(1)} %bitcast.108), channel_id=1, replica_groups=mesh['groups'=2,'adapter'=16,'tensor'=8] {'adapter'}, dimensions={0}, use_global_device_ids=true | all-gather | bytes 139264 | tf_op jit(solution)/shard_map/all_gather | solution.py:84
  101.2 4.5 %broadcast_multiply_fusion = f32[32,128,512]{2,1,0:T(8,128)} fusion(bf16[32,16,512]{2,1,0:T(8,128)(2,1)S(1)} %gather_fusion.3, pred[32]{0:T(512)(128)(4,1)S(1)} %get-tuple-element.7, bf16[4096,16]{0,1:T(8,128)(2,1)S(1)} %all_gather.11), kind=kOutput, calls=%fused_computation.6 | convolution fusion | flops 69468160 | bytes 9044000 | tf_op jit(solution)/shard_map/ksr,krf->ksf/dot_general | solution.py:87
  105.7 35.5 %all-gather.3.cloned.1.call-done = bf16[4096,1024]{1,0:T(8,128)(2,1)} async-done(((bf16[256,1024]{1,0:T(8,128)(2,1)}), bf16[4096,1024]{1,0:T(8,128)(2,1)}) %all-gather.3.cloned.1.call-update) | async-done | bytes 8388624 | tf_op jit(solution)/shard_map/all_gather | solution.py:83
  141.2 0.0 copy-done
  141.2 10.8 %fusion = bf16[4096,512]{1,0:T(8,128)(2,1)} fusion(f32[32,128,512]{2,1,0:T(8,128)} %broadcast_multiply_fusion, bf16[4096,1024]{1,0:T(8,128)(2,1)} %all-gather.3.cloned.1.call-done, bf16[1024,512]{1,0:T(8,128)(2,1)S(1)} %copy-done), kind=kOutput, calls=%fused_computation.5 | convolution fusion | flops 4299161600 | bytes 22020096 | tf_op jit(solution)/shard_map/dot_general | solution.py:85
  152.0 0.1 reduce-scatter.2.cloned.1.call-update
  152.0 55.6 %reduce-scatter.2.cloned.1.call-done = bf16[512,512]{1,0:T(8,128)(2,1)} async-done(((bf16[4096,512]{1,0:T(8,128)(2,1)}), bf16[512,512]{1,0:T(8,128)(2,1)}) %reduce-scatter.2.cloned.1.call-update) | async-done | bytes 524304 | tf_op jit(solution)/shard_map/reduce_scatter | solution.py:96
  (11 shorter events, 0.1 us)
Async XLA Ops:
  6.5 134.7 %copy-start = (bf16[1024,512]{1,0:T(8,128)(2,1)S(1)}, bf16[1024,512]{1,0:T(8,128)(2,1)}, u32[]{:S(2)}) copy-start(bf16[1024,512]{1,0:T(8,128)(2,1)} %param.8) | copy-start | bytes 3145732
  6.6 78.9 %copy-start.1 = (bf16[256,1024]{1,0:T(8,128)(2,1)S(1)}, bf16[256,1024]{1,0:T(8,128)(2,1)}, u32[]{:S(2)}) copy-start(bf16[256,1024]{1,0:T(8,128)(2,1)} %param.7) | copy-start | bytes 1572868
  6.6 43.1 %copy-start.2 = (s32[32]{0:T(128)S(1)}, s32[32]{0:T(128)}, u32[]{:S(2)}) copy-start(s32[32]{0:T(128)} %param.12) | copy-start | bytes 388
  6.6 76.7 %all-gather.5.cloned.1.call-start = ((), (), s32[]{:S(2)}) async-start(), calls=%async_computation.3 | async-start | bytes 2228224 | tf_op jit(solution)/shard_map/all_gather | solution.py:69
  10.8 130.4 %all-gather.3.cloned.1.call-start = ((), (), s32[]{:S(2)}) async-start(), calls=%async_computation.2 | async-start | bytes 8912896 | tf_op jit(solution)/shard_map/all_gather | solution.py:83
  25.7 56.9 %all-to-all-start = ((bf16[16,4,16,512]{3,2,1,0:T(8,128)(2,1)}), bf16[16,4,16,512]{3,2,1,0:T(8,128)(2,1)S(1)}, u32[]{:S(2)}, u32[]{:S(2)}) async-start(bf16[16,4,16,512]{3,2,1,0:T(8,128)(2,1)} %fusion.8), calls=%async_computation | async-start | bytes 2097152 | tf_op jit(solution)/shard_map/all_to_all | solution.py:58
  49.6 158.1 %reduce-scatter.2.cloned.1.call-start = ((), (), s32[]{:S(2)}) async-start(), calls=%async_computation.4 | async-start | bytes 4718592 | tf_op jit(solution)/shard_map/reduce_scatter | solution.py:96
Sparse Core Ops, SparseCore 0:
  10.9 72.3 all-gather.4
  85.1 56.0 all-gather.2
  152.2 55.4 reduce-scatter.1
